TPU v7x, 512 devices: a whole 4x8x8 slice. The times are simulated.
512 devices in a mesh: row: 64 (over z_lo, y, core), vec: 8 (over z_hi, x).
Axes of the slice: x: 4, y: 8, z: 8 (z_hi: 2, z_lo: 4; z = z_hi * 4 + z_lo), core: 2. Of those that a mesh axis runs over, the one named last changes fastest.
Arguments:
- eigvecs: float32 [32768, 8192], P('row', 'vec'), may hold values from -6 to 6
- reflectors: float32 [6, 32768, 128], P(None, 'row', 'vec'), may hold values from -0.375 to 0.375
- factors: float32 [6, 128, 128, 128], P(None, 'row', 'vec'), may hold values from -0.25 to 0.25
Outputs:
- vectors: float32 [32768, 8192], P('row', 'vec')
All inputs are finite; a program needn't handle non-finite values.
Results may differ from a plain program's by a relative error of at most 0.0001.
Values sent between devices are 32-bit elements; how exact they have to be, the bound alone decides.
No kernel may reach another device: no remote copies, remote signals or barrier semaphores. Data moves between devices by JAX's collectives and lax.ppermute only.
A program may use at most 64 MiB of HBM per device.

v0:
```python
import jax
import jax.numpy as jnp
from jax import lax
from jax.sharding import PartitionSpec as P

NB = 128
ROUNDS = 6
highest = lax.Precision.HIGHEST


def gather_turned(arrays, axis, dims):
    turned = [jnp.moveaxis(a, dim, 0) for a, dim in zip(arrays, dims)]
    widths = [t[0].size for t in turned]
    both = jnp.concatenate([t.reshape(-1, w) for t, w in zip(turned, widths)], axis=1)
    whole = lax.all_gather(both, axis, axis=0, tiled=True)
    blocks = jnp.split(whole, [sum(widths[:k]) for k in range(1, len(widths))], axis=1)
    return tuple(
        (
            jnp.moveaxis(b.reshape(-1, *t.shape[1:]), 0, dim)
            for b, t, dim in zip(blocks, turned, dims)
        )
    )


def passed_along(value, axis, steps):
    count = lax.axis_size(axis)
    initial, last = (max(0, -steps), min(count, count - steps))
    return lax.ppermute(value, axis, [(source, source + steps) for source in range(initial, last)])


def product(left, right):
    return jnp.dot(left, right, precision=highest, preferred_element_type=jnp.float32)


def apply_groups(panel, basis, blocks):
    inner = jnp.einsum("gri,grc->gic", basis, panel, precision=highest)
    images = jnp.einsum("gij,gjc->gic", blocks, inner, precision=highest)
    return panel - jnp.einsum("gri,gic->grc", basis, images, precision=highest)


def per_device(eigvecs, reflectors, factors):
    height = eigvecs.shape[0]
    width = eigvecs.shape[1]
    groups = height // (2 * NB)
    reach = (ROUNDS - 1) // 2
    basis_all, blocks_all = gather_turned((reflectors, factors), "vec", (2, 2))
    earlier = passed_along(blocks_all, "row", 1)
    slid = earlier[2:, groups - reach :]
    vectors = eigvecs
    for number in range(ROUNDS):
        behind = number // 2
        if behind > 0:
            blocks = jnp.concatenate(
                [slid[number - 2, reach - behind :], blocks_all[number, : groups - behind]], 0
            )
        else:
            blocks = blocks_all[number]
        basis = basis_all[number]
        if number % 2 == 0:
            panel = apply_groups(
                vectors.reshape(groups, 2 * NB, width), basis.reshape(groups, 2 * NB, NB), blocks
            )
            vectors = panel.reshape(height, width)
        else:
            head_rows = vectors[:NB]
            head_basis = basis[:NB]
            tail_rows = vectors[height - NB :]
            tail_basis = basis[height - NB :]
            last_block = blocks[groups - 1]
            head_inner = product(head_basis.T, head_rows)
            below = passed_along(head_inner, "row", -1)
            tail_inner = product(tail_basis.T, tail_rows) + below
            tail_image = product(last_block, tail_inner)
            above = passed_along(tail_image, "row", 1)
            head_new = head_rows - product(head_basis, above)
            tail_new = tail_rows - product(tail_basis, tail_image)
            middle = apply_groups(
                vectors[NB : height - NB].reshape(groups - 1, 2 * NB, width),
                basis[NB : height - NB].reshape(groups - 1, 2 * NB, NB),
                blocks[: groups - 1],
            ).reshape(height - 2 * NB, width)
            vectors = jnp.concatenate([head_new, middle, tail_new], 0)
    return vectors


def solution(mesh):
    return jax.shard_map(
        per_device,
        mesh=mesh,
        in_specs=(P("row", "vec"), P(None, "row", "vec"), P(None, "row", "vec", None)),
        out_specs=P("row", "vec"),
        check_vma=False,
    )
```

profile of v0, /device:TPU:64, one launch (start us, length us, event | category | flops | bytes accessed | tf_op | source)
XLA Modules:
  0.0 202.4 jit_solution(14676674547720633686)
XLA Ops:
  6.5 0.9 copy.15
  7.6 0.9 copy.25
  8.5 0.7 pad_maximum_fusion.3
  9.3 88.4 %all-gather.2.cloned.1.call-done = f32[128,4608]{1,0:T(8,128)} async-done(((f32[16,4608]{1,0:T(8,128)}), f32[128,4608]{1,0:T(8,128)}) %all-gather.2.cloned.1.call-update) | async-done | bytes 2359312 | tf_op jit(solution)/shard_map/all_gather | solution.py:15
  97.6 1.4 slice-done
  99.5 1.1 slice-done.1
  101.3 1.9 collective-permute-start.2
  103.2 3.1 %fusion.29 = f32[2,128,1024]{2,1,0:T(8,128)S(1)} fusion(f32[2,256,128]{2,1,0:T(8,128)S(1)} %bitcast.160, f32[2,256,1024]{2,1,0:T(8,128)} %bitcast.153), kind=kOutput, calls=%fused_computation.67 | convolution fusion | flops 805306368 | bytes 3407872 | tf_op jit(solution)/shard_map/gri,grc->gic/dot_general | solution.py:36
  106.3 1.0 fusion.16
  107.3 1.8 convolution_subtract_fusion.2
  109.1 0.7 fusion.4
  109.8 0.6 fusion.13
  110.5 5.8 %collective-permute-start = (f32[128,1024]{1,0:T(8,128)S(1)}, f32[128,1024]{1,0:T(8,128)S(1)}, u32[]{:S(2)}, u32[]{:S(2)}) collective-permute-start(f32[128,1024]{1,0:T(8,128)S(1)} %fusion.13), channel_id=1, source_target_pairs={{8,0},{16,8},{24,16},{32,24},{40,32},{48,40},{56,48},{64,56},{72,6... | collective-permute-start | bytes 1572872 | tf_op jit(solution)/shard_map/ppermute | solution.py:28
  116.8 1.0 convolution_subtract_fusion.5
  117.8 5.1 %collective-permute-done = f32[128,1024]{1,0:T(8,128)S(1)} collective-permute-done((f32[128,1024]{1,0:T(8,128)S(1)}, f32[128,1024]{1,0:T(8,128)S(1)}, u32[]{:S(2)}, u32[]{:S(2)}) %collective-permute-start) | collective-permute-done | bytes 524320 | tf_op jit(solution)/shard_map/ppermute | solution.py:28
  122.9 0.6 convolution_add_fusion.2
  124.1 2.1 %collective-permute-start.1 = (f32[128,1024]{1,0:T(8,128)S(1)}, f32[128,1024]{1,0:T(8,128)S(1)}, u32[]{:S(2)}, u32[]{:S(2)}) collective-permute-start(f32[128,1024]{1,0:T(8,128)S(1)} %fusion.26), channel_id=1, source_target_pairs={{0,8},{8,16},{16,24},{24,32},{32,40},{40,48},{48,56},{56,64},{64,7... | collective-permute-start | bytes 1572872 | tf_op jit(solution)/shard_map/ppermute | solution.py:28
  126.2 0.6 convolution_subtract_fusion.10
  126.9 10.0 %collective-permute-done.1 = f32[128,1024]{1,0:T(8,128)S(1)} collective-permute-done((f32[128,1024]{1,0:T(8,128)S(1)}, f32[128,1024]{1,0:T(8,128)S(1)}, u32[]{:S(2)}, u32[]{:S(2)}) %collective-permute-start.1) | collective-permute-done | bytes 524320 | tf_op jit(solution)/shard_map/ppermute | solution.py:28
  136.9 0.6 convolution_subtract_fusion.11
  137.7 1.3 fusion.30
  139.1 1.0 fusion.17
  140.1 1.9 convolution_subtract_fusion.1
  142.0 0.6 fusion.10
  142.6 1.9 collective-permute-start.3
  144.5 0.7 fusion.2
  145.8 5.4 %collective-permute-done.3 = f32[128,1024]{1,0:T(8,128)S(1)} collective-permute-done((f32[128,1024]{1,0:T(8,128)S(1)}, f32[128,1024]{1,0:T(8,128)S(1)}, u32[]{:S(2)}, u32[]{:S(2)}) %collective-permute-start.3) | collective-permute-done | bytes 524320 | tf_op jit(solution)/shard_map/ppermute | solution.py:28
  151.2 0.6 convolution_add_fusion.1
  151.8 0.6 fusion.24
  152.4 2.1 %collective-permute-start.4 = (f32[128,1024]{1,0:T(8,128)S(1)}, f32[128,1024]{1,0:T(8,128)S(1)}, u32[]{:S(2)}, u32[]{:S(2)}) collective-permute-start(f32[128,1024]{1,0:T(8,128)S(1)} %fusion.24), channel_id=1, source_target_pairs={{0,8},{8,16},{16,24},{24,32},{32,40},{40,48},{48,56},{56,64},{64,7... | collective-permute-start | bytes 1572872 | tf_op jit(solution)/shard_map/ppermute | solution.py:28
  154.6 1.0 convolution_subtract_fusion.4
  155.6 0.6 convolution_subtract_fusion.8
  156.2 9.0 %collective-permute-done.4 = f32[128,1024]{1,0:T(8,128)S(1)} collective-permute-done((f32[128,1024]{1,0:T(8,128)S(1)}, f32[128,1024]{1,0:T(8,128)S(1)}, u32[]{:S(2)}, u32[]{:S(2)}) %collective-permute-start.4) | collective-permute-done | bytes 524320 | tf_op jit(solution)/shard_map/ppermute | solution.py:28
  165.2 0.6 convolution_subtract_fusion.9
  166.1 1.3 fusion.31
  167.4 1.0 fusion.15
  168.4 1.9 convolution_subtract_fusion
  170.3 0.6 fusion.7
  170.9 1.9 collective-permute-start.5
  172.8 0.7 fusion
  174.2 5.4 %collective-permute-done.5 = f32[128,1024]{1,0:T(8,128)S(1)} collective-permute-done((f32[128,1024]{1,0:T(8,128)S(1)}, f32[128,1024]{1,0:T(8,128)S(1)}, u32[]{:S(2)}, u32[]{:S(2)}) %collective-permute-start.5) | collective-permute-done | bytes 524320 | tf_op jit(solution)/shard_map/ppermute | solution.py:28
  179.5 0.6 convolution_add_fusion
  180.7 1.9 collective-permute-start.6
  182.7 1.0 convolution_subtract_fusion.3
  183.7 0.6 convolution_subtract_fusion.6
  184.3 9.2 %collective-permute-done.6 = f32[128,1024]{1,0:T(8,128)S(1)} collective-permute-done((f32[128,1024]{1,0:T(8,128)S(1)}, f32[128,1024]{1,0:T(8,128)S(1)}, u32[]{:S(2)}, u32[]{:S(2)}) %collective-permute-start.6) | collective-permute-done | bytes 524320 | tf_op jit(solution)/shard_map/ppermute | solution.py:28
  193.5 0.6 convolution_subtract_fusion.7
  194.1 1.5 pad_maximum_fusion.2
  (21 shorter events, 4.5 us)
Async XLA Ops:
  6.5 91.1 %all-gather.2.cloned.1.call-start = ((), (), s32[]{:S(2)}) async-start(), calls=%async_computation | async-start | bytes 2654208 | tf_op jit(solution)/shard_map/all_gather | solution.py:15
  97.6 1.4 slice-start
  99.5 1.1 slice-start.1
  101.3 25.6 %collective-permute-start.2 = (f32[6,2,128,128]{3,2,1,0:T(8,128)S(1)}, f32[6,2,128,128]{3,2,1,0:T(8,128)S(1)}, u32[]{:S(2)}, u32[]{:S(2)}) collective-permute-start(f32[6,2,128,128]{3,2,1,0:T(8,128)S(1)} %bitcast.162), channel_id=1, source_target_pairs={{0,8},{8,16},{16,24},{24,32},{32,40},{40,48},{48,56},{56,64},{64,7... | collective-permute-start | bytes 2359304 | tf_op jit(solution)/shard_map/ppermute | solution.py:28
  103.2 4.1 %copy-start = (f32[512,1024]{1,0:T(8,128)S(1)}, f32[512,1024]{1,0:T(8,128)}, u32[]{:S(2)}) copy-start(f32[512,1024]{1,0:T(8,128)} %param.3) | copy-start | bytes 6291460
  110.5 12.4 %collective-permute-start = (f32[128,1024]{1,0:T(8,128)S(1)}, f32[128,1024]{1,0:T(8,128)S(1)}, u32[]{:S(2)}, u32[]{:S(2)}) collective-permute-start(f32[128,1024]{1,0:T(8,128)S(1)} %fusion.13), channel_id=1, source_target_pairs={{8,0},{16,8},{24,16},{32,24},{40,32},{48,40},{56,48},{64,56},{72,6... | collective-permute-start | bytes 1572872 | tf_op jit(solution)/shard_map/ppermute | solution.py:28
  124.1 12.8 %collective-permute-start.1 = (f32[128,1024]{1,0:T(8,128)S(1)}, f32[128,1024]{1,0:T(8,128)S(1)}, u32[]{:S(2)}, u32[]{:S(2)}) collective-permute-start(f32[128,1024]{1,0:T(8,128)S(1)} %fusion.26), channel_id=1, source_target_pairs={{0,8},{8,16},{16,24},{24,32},{32,40},{40,48},{48,56},{56,64},{64,7... | collective-permute-start | bytes 1572872 | tf_op jit(solution)/shard_map/ppermute | solution.py:28
  142.6 8.6 %collective-permute-start.3 = (f32[128,1024]{1,0:T(8,128)S(1)}, f32[128,1024]{1,0:T(8,128)S(1)}, u32[]{:S(2)}, u32[]{:S(2)}) collective-permute-start(f32[128,1024]{1,0:T(8,128)S(1)} %fusion.10), channel_id=1, source_target_pairs={{8,0},{16,8},{24,16},{32,24},{40,32},{48,40},{56,48},{64,56},{72,6... | collective-permute-start | bytes 1572872 | tf_op jit(solution)/shard_map/ppermute | solution.py:28
  152.4 12.8 %collective-permute-start.4 = (f32[128,1024]{1,0:T(8,128)S(1)}, f32[128,1024]{1,0:T(8,128)S(1)}, u32[]{:S(2)}, u32[]{:S(2)}) collective-permute-start(f32[128,1024]{1,0:T(8,128)S(1)} %fusion.24), channel_id=1, source_target_pairs={{0,8},{8,16},{16,24},{24,32},{32,40},{40,48},{48,56},{56,64},{64,7... | collective-permute-start | bytes 1572872 | tf_op jit(solution)/shard_map/ppermute | solution.py:28
  170.9 8.6 %collective-permute-start.5 = (f32[128,1024]{1,0:T(8,128)S(1)}, f32[128,1024]{1,0:T(8,128)S(1)}, u32[]{:S(2)}, u32[]{:S(2)}) collective-permute-start(f32[128,1024]{1,0:T(8,128)S(1)} %fusion.7), channel_id=1, source_target_pairs={{8,0},{16,8},{24,16},{32,24},{40,32},{48,40},{56,48},{64,56},{72,6... | collective-permute-start | bytes 1572872 | tf_op jit(solution)/shard_map/ppermute | solution.py:28
  180.7 12.8 %collective-permute-start.6 = (f32[128,1024]{1,0:T(8,128)S(1)}, f32[128,1024]{1,0:T(8,128)S(1)}, u32[]{:S(2)}, u32[]{:S(2)}) collective-permute-start(f32[128,1024]{1,0:T(8,128)S(1)} %fusion.22), channel_id=1, source_target_pairs={{0,8},{8,16},{16,24},{24,32},{32,40},{40,48},{48,56},{56,64},{64,7... | collective-permute-start | bytes 1572872 | tf_op jit(solution)/shard_map/ppermute | solution.py:28
Sparse Core Ops, SparseCore 0:
  10.5 87.0 all-gather.1
where the time goes:
time: 203 us; the launch traced here: 202 us
  waiting for transfers between devices  132 us (65%)
  matrix products  30.2 us (15%)
  starting transfers between devices  17.7 us (9%)
  between operations  13.8 us (7%)
  local copies, waits for them, and re-layouts  5.56 us (3%)
  other arithmetic  2.67 us (1%)
    all_gather x1, waiting for transfers between devices, gather_turned(): whole = lax.all_gather(both, axis, axis=0, tiled=True)  88.4 us
    ppermute x7, waiting for transfers between devices, passed_along(): lax.ppermute(value, axis, [(source, source + steps) for source in range(i...  44.1 us
    ppermute x7, starting transfers between devices, passed_along(): lax.ppermute(value, axis, [(source, source + steps) for source in range(i...  17.7 us
    dot_general x15, matrix products, product(): jnp.dot(left, right, precision=highest, preferred_element_type=jnp.float32)  9.06 us
    dot_general x6, matrix products, apply_groups(): return panel - jnp.einsum('gri,gic->grc', basis, images, precision=highest)  8.62 us
    dot_general x6, matrix products, apply_groups(): inner = jnp.einsum('gri,grc->gic', basis, panel, precision=highest)  7.84 us
    dot_general x6, matrix products, apply_groups(): images = jnp.einsum('gij,gjc->gic', blocks, inner, precision=highest)  4.71 us
  transfers between devices with their start and end apart: 8, of which 7 were waited for; matrix products, arithmetic and copies ran while one was open for 8% of the time, Pallas kernels for 0%

commit v1 on v0

--- a/solution.py
+++ b/solution.py
@@ -12,7 +12,8 @@
     turned = [jnp.moveaxis(a, dim, 0) for a, dim in zip(arrays, dims)]
     widths = [t[0].size for t in turned]
     both = jnp.concatenate([t.reshape(-1, w) for t, w in zip(turned, widths)], axis=1)
-    whole = lax.all_gather(both, axis, axis=0, tiled=True)
+    stack = jnp.stack([both] * lax.axis_size(axis))
+    whole = jnp.concatenate(lax.all_to_all(stack, axis, 0, 0), axis=0)
     blocks = jnp.split(whole, [sum(widths[:k]) for k in range(1, len(widths))], axis=1)
     return tuple(
         (

time: 203 us -> 171 us (0.84)
  waiting for transfers between devices: 132 us -> 44.1 us
  blocking collectives: 0 us -> 70.5 us
  between operations: 13.8 us -> 0.44 us
    all_gather x1 -> x0, waiting for transfers between devices: 88.4 us -> none  [gather_turned(): whole = lax.all_gather(both, axis, axis=0, tiled=True)]
    all_to_all x0 -> x1, blocking collectives: none -> 70.5 us  [gather_turned(): whole = jnp.concatenate(lax.all_to_all(stack, axis, 0, 0), axis=0)]
  transfers between devices with their start and end apart: 8 -> 7, of which waited for: 7 -> 6; matrix products, arithmetic and copies ran while one was open for 8% -> 10% of each run, Pallas kernels for 0% -> 0%
where the time goes in v1:
time: 171 us; the launch traced here: 170 us
  blocking collectives  70.5 us (41%)
  waiting for transfers between devices  44.1 us (26%)
  matrix products  30.2 us (18%)
  starting transfers between devices  17.7 us (10%)
  local copies, waits for them, and re-layouts  5.42 us (3%)
  other arithmetic  1.95 us (1%)
    all_to_all x1, blocking collectives, gather_turned(): whole = jnp.concatenate(lax.all_to_all(stack, axis, 0, 0), axis=0)  70.5 us
    ppermute x7, waiting for transfers between devices, passed_along(): lax.ppermute(value, axis, [(source, source + steps) for source in range(i...  44.1 us
    ppermute x7, starting transfers between devices, passed_along(): lax.ppermute(value, axis, [(source, source + steps) for source in range(i...  17.7 us
    dot_general x15, matrix products, product(): jnp.dot(left, right, precision=highest, preferred_element_type=jnp.float32)  9.06 us
    dot_general x6, matrix products, apply_groups(): return panel - jnp.einsum('gri,gic->grc', basis, images, precision=highest)  8.62 us
    dot_general x6, matrix products, apply_groups(): inner = jnp.einsum('gri,grc->gic', basis, panel, precision=highest)  7.84 us
    dot_general x6, matrix products, apply_groups(): images = jnp.einsum('gij,gjc->gic', blocks, inner, precision=highest)  4.71 us
  transfers between devices with their start and end apart: 7, of which 6 were waited for; matrix products, arithmetic and copies ran while one was open for 10% of the time, Pallas kernels for 0%

profile of v1, /device:TPU:64, one launch (start us, length us, event | category | flops | bytes accessed | tf_op | source)
XLA Modules:
  0.0 170.4 jit_solution(7680173677217426416)
XLA Ops:
  0.0 0.9 copy.15
  1.0 0.9 copy.25
  2.2 70.5 %all_to_all.5 = f32[8,16,4608]{2,1,0:T(8,128)S(1)} all-to-all(f32[8,16,4608]{2,1,0:T(8,128)S(1)} %stack.2), channel_id=1, replica_groups=mesh['row'=64,'vec'=8] {'vec'}, dimensions={0} | all-to-all | bytes 4718592 | tf_op jit(solution)/shard_map/all_to_all | solution.py:16
  72.8 0.9 split.9
  74.3 1.4 copy.17
  76.0 1.9 %collective-permute-start.2 = (f32[6,2,128,128]{3,2,1,0:T(8,128)S(1)}, f32[6,2,128,128]{3,2,1,0:T(8,128)S(1)}, u32[]{:S(2)}, u32[]{:S(2)}) collective-permute-start(f32[6,2,128,128]{3,2,1,0:T(8,128)S(1)} %bitcast.165), channel_id=1, source_target_pairs={{0,8},{8,16},{16,24},{24,32},{32,40},{40,48},{48,56},{56,64},{64,7... | collective-permute-start | bytes 2359304 | tf_op jit(solution)/shard_map/ppermute | solution.py:29
  78.0 3.1 %fusion.29 = f32[2,128,1024]{2,1,0:T(8,128)S(1)} fusion(f32[2,256,128]{2,1,0:T(8,128)S(1)} %bitcast.163, f32[2,256,1024]{2,1,0:T(8,128)} %bitcast.156), kind=kOutput, calls=%fused_computation.67 | convolution fusion | flops 805306368 | bytes 3407872 | tf_op jit(solution)/shard_map/gri,grc->gic/dot_general | solution.py:37
  81.0 1.0 fusion.16
  82.0 1.8 %convolution_subtract_fusion.2 = f32[2,256,1024]{2,1,0:T(8,128)S(1)} fusion(f32[2,256,1024]{2,1,0:T(8,128)S(1)} %bitcast.157, f32[2,256,128]{2,1,0:T(8,128)S(1)} %bitcast.164, f32[2,128,1024]{2,1,0:T(8,128)S(1)} %fusion.16), kind=kOutput, calls=%fused_computation.5 | convolution fusion | flops 805830656 | bytes 5505024 | tf_op jit(solution)/shard_map/gri,gic->grc/dot_general | solution.py:39
  83.9 0.7 fusion.4
  84.6 0.6 fusion.13
  85.2 5.7 %collective-permute-start = (f32[128,1024]{1,0:T(8,128)S(1)}, f32[128,1024]{1,0:T(8,128)S(1)}, u32[]{:S(2)}, u32[]{:S(2)}) collective-permute-start(f32[128,1024]{1,0:T(8,128)S(1)} %fusion.13), channel_id=1, source_target_pairs={{8,0},{16,8},{24,16},{32,24},{40,32},{48,40},{56,48},{64,56},{72,6... | collective-permute-start | bytes 1572872 | tf_op jit(solution)/shard_map/ppermute | solution.py:29
  91.0 0.6 fusion.25
  91.6 1.0 convolution_subtract_fusion.5
  92.6 5.1 %collective-permute-done = f32[128,1024]{1,0:T(8,128)S(1)} collective-permute-done((f32[128,1024]{1,0:T(8,128)S(1)}, f32[128,1024]{1,0:T(8,128)S(1)}, u32[]{:S(2)}, u32[]{:S(2)}) %collective-permute-start) | collective-permute-done | bytes 524320 | tf_op jit(solution)/shard_map/ppermute | solution.py:29
  97.7 0.6 convolution_add_fusion.2
  98.9 2.1 %collective-permute-start.1 = (f32[128,1024]{1,0:T(8,128)S(1)}, f32[128,1024]{1,0:T(8,128)S(1)}, u32[]{:S(2)}, u32[]{:S(2)}) collective-permute-start(f32[128,1024]{1,0:T(8,128)S(1)} %fusion.26), channel_id=1, source_target_pairs={{0,8},{8,16},{16,24},{24,32},{32,40},{40,48},{48,56},{56,64},{64,7... | collective-permute-start | bytes 1572872 | tf_op jit(solution)/shard_map/ppermute | solution.py:29
  101.0 0.6 convolution_subtract_fusion.10
  101.6 10.0 %collective-permute-done.1 = f32[128,1024]{1,0:T(8,128)S(1)} collective-permute-done((f32[128,1024]{1,0:T(8,128)S(1)}, f32[128,1024]{1,0:T(8,128)S(1)}, u32[]{:S(2)}, u32[]{:S(2)}) %collective-permute-start.1) | collective-permute-done | bytes 524320 | tf_op jit(solution)/shard_map/ppermute | solution.py:29
  111.7 0.6 convolution_subtract_fusion.11
  112.5 1.3 fusion.30
  113.8 1.0 fusion.17
  114.8 1.9 %convolution_subtract_fusion.1 = f32[2,256,1024]{2,1,0:T(8,128)S(1)} fusion(f32[2,256,1024]{2,1,0:T(8,128)S(1)} %bitcast.132, f32[2,256,128]{2,1,0:T(8,128)S(1)} %bitcast.162, f32[2,128,1024]{2,1,0:T(8,128)S(1)} %fusion.17), kind=kOutput, calls=%fused_computation.4 | convolution fusion | flops 805830656 | bytes 5505024 | tf_op jit(solution)/shard_map/gri,gic->grc/dot_general | solution.py:39
  116.7 0.6 fusion.10
  117.4 1.9 %collective-permute-start.3 = (f32[128,1024]{1,0:T(8,128)S(1)}, f32[128,1024]{1,0:T(8,128)S(1)}, u32[]{:S(2)}, u32[]{:S(2)}) collective-permute-start(f32[128,1024]{1,0:T(8,128)S(1)} %fusion.10), channel_id=1, source_target_pairs={{8,0},{16,8},{24,16},{32,24},{40,32},{48,40},{56,48},{64,56},{72,6... | collective-permute-start | bytes 1572872 | tf_op jit(solution)/shard_map/ppermute | solution.py:29
  119.3 0.7 fusion.2
  120.6 5.4 %collective-permute-done.3 = f32[128,1024]{1,0:T(8,128)S(1)} collective-permute-done((f32[128,1024]{1,0:T(8,128)S(1)}, f32[128,1024]{1,0:T(8,128)S(1)}, u32[]{:S(2)}, u32[]{:S(2)}) %collective-permute-start.3) | collective-permute-done | bytes 524320 | tf_op jit(solution)/shard_map/ppermute | solution.py:29
  126.0 0.6 convolution_add_fusion.1
  126.6 0.6 fusion.24
  127.2 2.1 %collective-permute-start.4 = (f32[128,1024]{1,0:T(8,128)S(1)}, f32[128,1024]{1,0:T(8,128)S(1)}, u32[]{:S(2)}, u32[]{:S(2)}) collective-permute-start(f32[128,1024]{1,0:T(8,128)S(1)} %fusion.24), channel_id=1, source_target_pairs={{0,8},{8,16},{16,24},{24,32},{32,40},{40,48},{48,56},{56,64},{64,7... | collective-permute-start | bytes 1572872 | tf_op jit(solution)/shard_map/ppermute | solution.py:29
  129.4 1.0 convolution_subtract_fusion.4
  130.4 0.6 convolution_subtract_fusion.8
  131.0 9.0 %collective-permute-done.4 = f32[128,1024]{1,0:T(8,128)S(1)} collective-permute-done((f32[128,1024]{1,0:T(8,128)S(1)}, f32[128,1024]{1,0:T(8,128)S(1)}, u32[]{:S(2)}, u32[]{:S(2)}) %collective-permute-start.4) | collective-permute-done | bytes 524320 | tf_op jit(solution)/shard_map/ppermute | solution.py:29
  140.0 0.6 convolution_subtract_fusion.9
  140.8 1.3 fusion.31
  142.2 1.0 fusion.15
  143.1 1.9 %convolution_subtract_fusion = f32[2,256,1024]{2,1,0:T(8,128)S(1)} fusion(f32[2,256,1024]{2,1,0:T(8,128)S(1)} %bitcast.134, f32[2,256,128]{2,1,0:T(8,128)S(1)} %bitcast.160, f32[2,128,1024]{2,1,0:T(8,128)S(1)} %fusion.15), kind=kOutput, calls=%fused_computation.3 | convolution fusion | flops 805830656 | bytes 5505024 | tf_op jit(solution)/shard_map/gri,gic->grc/dot_general | solution.py:39
  145.0 0.6 fusion.7
  145.7 1.9 %collective-permute-start.5 = (f32[128,1024]{1,0:T(8,128)S(1)}, f32[128,1024]{1,0:T(8,128)S(1)}, u32[]{:S(2)}, u32[]{:S(2)}) collective-permute-start(f32[128,1024]{1,0:T(8,128)S(1)} %fusion.7), channel_id=1, source_target_pairs={{8,0},{16,8},{24,16},{32,24},{40,32},{48,40},{56,48},{64,56},{72,6... | collective-permute-start | bytes 1572872 | tf_op jit(solution)/shard_map/ppermute | solution.py:29
  147.6 0.7 fusion
  148.9 5.4 %collective-permute-done.5 = f32[128,1024]{1,0:T(8,128)S(1)} collective-permute-done((f32[128,1024]{1,0:T(8,128)S(1)}, f32[128,1024]{1,0:T(8,128)S(1)}, u32[]{:S(2)}, u32[]{:S(2)}) %collective-permute-start.5) | collective-permute-done | bytes 524320 | tf_op jit(solution)/shard_map/ppermute | solution.py:29
  154.3 0.6 convolution_add_fusion
  155.5 1.9 %collective-permute-start.6 = (f32[128,1024]{1,0:T(8,128)S(1)}, f32[128,1024]{1,0:T(8,128)S(1)}, u32[]{:S(2)}, u32[]{:S(2)}) collective-permute-start(f32[128,1024]{1,0:T(8,128)S(1)} %fusion.22), channel_id=1, source_target_pairs={{0,8},{8,16},{16,24},{24,32},{32,40},{40,48},{48,56},{56,64},{64,7... | collective-permute-start | bytes 1572872 | tf_op jit(solution)/shard_map/ppermute | solution.py:29
  157.4 1.0 convolution_subtract_fusion.3
  158.5 0.6 convolution_subtract_fusion.6
  159.1 9.2 %collective-permute-done.6 = f32[128,1024]{1,0:T(8,128)S(1)} collective-permute-done((f32[128,1024]{1,0:T(8,128)S(1)}, f32[128,1024]{1,0:T(8,128)S(1)}, u32[]{:S(2)}, u32[]{:S(2)}) %collective-permute-start.6) | collective-permute-done | bytes 524320 | tf_op jit(solution)/shard_map/ppermute | solution.py:29
  168.3 0.6 convolution_subtract_fusion.7
  168.9 1.5 pad_maximum_fusion.2
  (18 shorter events, 4.0 us)
Async XLA Ops:
  76.0 25.6 %collective-permute-start.2 = (f32[6,2,128,128]{3,2,1,0:T(8,128)S(1)}, f32[6,2,128,128]{3,2,1,0:T(8,128)S(1)}, u32[]{:S(2)}, u32[]{:S(2)}) collective-permute-start(f32[6,2,128,128]{3,2,1,0:T(8,128)S(1)} %bitcast.165), channel_id=1, source_target_pairs={{0,8},{8,16},{16,24},{24,32},{32,40},{40,48},{48,56},{56,64},{64,7... | collective-permute-start | bytes 2359304 | tf_op jit(solution)/shard_map/ppermute | solution.py:29
  78.0 4.1 %copy-start = (f32[512,1024]{1,0:T(8,128)S(1)}, f32[512,1024]{1,0:T(8,128)}, u32[]{:S(2)}) copy-start(f32[512,1024]{1,0:T(8,128)} %param.3) | copy-start | bytes 6291460
  85.2 12.4 %collective-permute-start = (f32[128,1024]{1,0:T(8,128)S(1)}, f32[128,1024]{1,0:T(8,128)S(1)}, u32[]{:S(2)}, u32[]{:S(2)}) collective-permute-start(f32[128,1024]{1,0:T(8,128)S(1)} %fusion.13), channel_id=1, source_target_pairs={{8,0},{16,8},{24,16},{32,24},{40,32},{48,40},{56,48},{64,56},{72,6... | collective-permute-start | bytes 1572872 | tf_op jit(solution)/shard_map/ppermute | solution.py:29
  98.9 12.8 %collective-permute-start.1 = (f32[128,1024]{1,0:T(8,128)S(1)}, f32[128,1024]{1,0:T(8,128)S(1)}, u32[]{:S(2)}, u32[]{:S(2)}) collective-permute-start(f32[128,1024]{1,0:T(8,128)S(1)} %fusion.26), channel_id=1, source_target_pairs={{0,8},{8,16},{16,24},{24,32},{32,40},{40,48},{48,56},{56,64},{64,7... | collective-permute-start | bytes 1572872 | tf_op jit(solution)/shard_map/ppermute | solution.py:29
  117.4 8.6 %collective-permute-start.3 = (f32[128,1024]{1,0:T(8,128)S(1)}, f32[128,1024]{1,0:T(8,128)S(1)}, u32[]{:S(2)}, u32[]{:S(2)}) collective-permute-start(f32[128,1024]{1,0:T(8,128)S(1)} %fusion.10), channel_id=1, source_target_pairs={{8,0},{16,8},{24,16},{32,24},{40,32},{48,40},{56,48},{64,56},{72,6... | collective-permute-start | bytes 1572872 | tf_op jit(solution)/shard_map/ppermute | solution.py:29
  127.2 12.8 %collective-permute-start.4 = (f32[128,1024]{1,0:T(8,128)S(1)}, f32[128,1024]{1,0:T(8,128)S(1)}, u32[]{:S(2)}, u32[]{:S(2)}) collective-permute-start(f32[128,1024]{1,0:T(8,128)S(1)} %fusion.24), channel_id=1, source_target_pairs={{0,8},{8,16},{16,24},{24,32},{32,40},{40,48},{48,56},{56,64},{64,7... | collective-permute-start | bytes 1572872 | tf_op jit(solution)/shard_map/ppermute | solution.py:29
  145.7 8.6 %collective-permute-start.5 = (f32[128,1024]{1,0:T(8,128)S(1)}, f32[128,1024]{1,0:T(8,128)S(1)}, u32[]{:S(2)}, u32[]{:S(2)}) collective-permute-start(f32[128,1024]{1,0:T(8,128)S(1)} %fusion.7), channel_id=1, source_target_pairs={{8,0},{16,8},{24,16},{32,24},{40,32},{48,40},{56,48},{64,56},{72,6... | collective-permute-start | bytes 1572872 | tf_op jit(solution)/shard_map/ppermute | solution.py:29
  155.5 12.8 %collective-permute-start.6 = (f32[128,1024]{1,0:T(8,128)S(1)}, f32[128,1024]{1,0:T(8,128)S(1)}, u32[]{:S(2)}, u32[]{:S(2)}) collective-permute-start(f32[128,1024]{1,0:T(8,128)S(1)} %fusion.22), channel_id=1, source_target_pairs={{0,8},{8,16},{16,24},{24,32},{32,40},{40,48},{48,56},{56,64},{64,7... | collective-permute-start | bytes 1572872 | tf_op jit(solution)/shard_map/ppermute | solution.py:29
